TPU v7x, 32 devices: a whole 2x2x4 slice. The times are simulated.
32 devices in a mesh: ang: 16 (over z, y, core), sl: 2 (over x).
Axes of the slice: x: 2, y: 2, z: 4, core: 2. Of those that a mesh axis runs over, the one named last changes fastest.
Arguments:
- sinogram: bfloat16 [16, 32, 1024], P('sl', 'ang'), may hold values from -72 to 72
- detector_coord: int32 [32, 32, 512], P('ang', 'sl'), may hold values from 0 to 1072693247
Outputs:
- image_rows: float32 [32, 16, 512], P('ang', 'sl')
All inputs are finite; a program needn't handle non-finite values.
Results may differ from a plain program's by a relative error of at most 0.0052.
Values may be sent and summed in bfloat16 or wider, within the bound.
A program may use at most 64 MiB of HBM per device.

v0:
```python
import functools
import math

import jax
import jax.numpy as jnp
from jax import lax
from jax.experimental import pallas as pl
from jax.experimental.pallas import tpu as pltpu
from jax.sharding import PartitionSpec as P

LANES = 128
FRACTION_BITS = 20


def ramp_block(size, shift):
    first = lax.broadcasted_iota(jnp.int32, (size, size), 0)
    second = lax.broadcasted_iota(jnp.int32, (size, size), 1)
    offset = second - first + shift
    offset_sq = jnp.maximum((offset * offset).astype(jnp.float32), jnp.float32(1.0))
    values = jnp.where(
        offset == 0,
        jnp.float32(0.25),
        jnp.where(
            (offset & 1) != 0, jnp.float32(-1.0 / math.pi**2) / offset_sq, jnp.float32(0.0)
        ),
    )
    return values.astype(jnp.bfloat16)


def build_ramp(ramp, size, count):
    for step in range(2 * count - 1):
        ramp[step] = ramp_block(size, (step - count + 1) * size)


def filter_rows(sino, ramp, tiles, size, count):
    rows = sino.shape[0] * sino.shape[1]
    per_row = sino.shape[2] // LANES
    for out_block in range(count):
        total = None
        for in_block in range(count):
            part = jnp.dot(
                sino[:, :, in_block * size : (in_block + 1) * size].reshape(rows, size),
                ramp[out_block - in_block + count - 1],
                preferred_element_type=jnp.float32,
            )
            total = part if total is None else total + part
        total = total.astype(jnp.bfloat16).astype(jnp.float32)
        for piece in range(size // LANES):
            h = out_block * (size // LANES) + piece
            tiles[pl.ds(h, rows, stride=per_row), :] = total[:, piece * LANES : (piece + 1) * LANES]


def pick(tile, index):
    return jnp.take_along_axis(tile, index, axis=1, mode="promise_in_bounds")


def interpolate(coords, tiles, out, scale, own_angles, together=2):
    rows, slices, width = out.shape
    groups = coords.shape[0]
    per_row = tiles.shape[0] // (groups * slices * own_angles)
    across = width // LANES
    level = lax.broadcasted_iota(jnp.int32, (per_row, LANES), 0)
    spots = [(r, x) for r in range(rows) for x in range(across)]
    for start in range(0, len(spots), together):
        group = spots[start : start + together]

        def one_group(g, sums):
            sums = list(sums)
            for al in range(own_angles):
                picks = []
                for r, x in group:
                    c = coords[g, pl.ds((al * rows + r) * across + x, 1), :]
                    c = jnp.broadcast_to(c, (per_row, LANES))
                    left = c >> FRACTION_BITS
                    right = left + 1
                    fraction = (c & (2**FRACTION_BITS - 1)).astype(jnp.float32) * jnp.float32(
                        2.0**-FRACTION_BITS
                    )
                    w_left = (1.0 - fraction).astype(jnp.bfloat16).astype(jnp.float32)
                    w_right = fraction.astype(jnp.bfloat16).astype(jnp.float32)
                    w_left = jnp.where(left >> 7 == level, w_left, 0.0)
                    w_right = jnp.where(right >> 7 == level, w_right, 0.0)
                    picks.append((left & (LANES - 1), right & (LANES - 1), w_left, w_right))
                held = []
                for s in range(slices):
                    row = ((g * slices + s) * own_angles + al) * per_row
                    held.append(tiles[pl.ds(pl.multiple_of(row, per_row), per_row), :])
                for i, (i_left, i_right, w_left, w_right) in enumerate(picks):
                    for index, weight in ((i_left, w_left), (i_right, w_right)):
                        for s in range(slices):
                            at = s * len(group) + i
                            sums[at] = sums[at] + weight * pick(held[s], index)
            return tuple(sums)

        zero = jnp.zeros((per_row, LANES), jnp.float32)
        sums = lax.fori_loop(0, groups, one_group, (zero,) * (slices * len(group)))
        for s in range(slices):
            for i, (r, x) in enumerate(group):
                line = jnp.sum(sums[s * len(group) + i], axis=0, keepdims=True) * scale
                out[r, pl.ds(s, 1), pl.ds(x * LANES, LANES)] = line


def kernel(
    groups, halves, own_angles, sino, coords, out, all_sino, all_coords, ramp, tiles,
    local_sem, s_send, n_send, f_send, s_recv, c_send, x_send, c_recv,
):
    me, half = lax.axis_index("ang"), lax.axis_index("sl")
    outer, outers = me // 4, groups // 4
    mate = me + 1 - 2 * (me % 2)
    near = me + 2 - 4 * (me // 2 % 2)
    total = groups * halves
    share = coords.shape[0]

    barrier = pltpu.get_barrier_semaphore()

    def greet(k, carry):
        there = lax.rem(me * halves + half + k, total)
        pl.semaphore_signal(
            barrier, inc=1, device_id={"ang": there // halves, "sl": there % halves},
            device_id_type=pl.DeviceIdType.MESH,
        )
        return carry

    lax.fori_loop(1, total, greet, 0)
    own = pltpu.make_async_copy(sino, all_sino.at[me], local_sem.at[0])
    own.start()
    bins, size = sino.shape[1], ramp.shape[1]
    build_ramp(ramp, size, bins // size)
    pl.semaphore_wait(barrier, total - 1)

    def sino_copy(block, target, send_sem, source=None):
        return pltpu.make_async_remote_copy(
            src_ref=all_sino.at[block] if source is None else source,
            dst_ref=all_sino.at[block], send_sem=send_sem,
            recv_sem=s_recv.at[block], device_id={"ang": target},
            device_id_type=pl.DeviceIdType.MESH,
        )

    def coord_copy(block, target, side, send_sem, source=None):
        return pltpu.make_async_remote_copy(
            src_ref=all_coords.at[block] if source is None else source,
            dst_ref=all_coords.at[block], send_sem=send_sem,
            recv_sem=c_recv.at[block], device_id={"ang": target, "sl": side},
            device_id_type=pl.DeviceIdType.MESH,
        )

    def far(k):
        return lax.rem(outer + k, outers) * 4 + me % 4

    primary = me // share == half
    for k in range(1, outers):
        sino_copy(me, far(k), s_send.at[k], sino).start()
    sino_copy(me, near, n_send.at[0], sino).start()
    sino_copy(me, mate, f_send.at[0], sino).start()
    for j in range(1, share):
        place = lax.rem(me + j, share)
        coord_copy(me, half * share + place, half, c_send.at[j], coords.at[place]).start()
    home = lax.rem(me, share)

    @pl.when(primary)
    def _():
        pltpu.make_async_copy(coords.at[home], all_coords.at[me], c_recv.at[me]).start()

    @pl.when(jnp.logical_not(primary))
    def _():
        coord_copy(me, half * share + home, half, c_send.at[0], coords.at[home]).start()

    def arrived(block):
        sino_copy(block, mate, s_send.at[0]).wait_recv()

    for k in range(1, outers):
        arrived(far(k))
        sino_copy(far(k), near, n_send.at[k]).start()
        sino_copy(far(k), mate, f_send.at[k]).start()

    def coords_arrived(g):
        pltpu.make_async_copy(coords.at[0], all_coords.at[g], c_recv.at[g]).wait()

    def spread(g):
        coords_arrived(g)
        for t in range(1, halves):
            side = lax.rem(half + t, halves)
            coord_copy(g, me, side, x_send.at[g * (halves - 1) + t - 1]).start()

    def from_near(k):
        return lax.rem(outer + k, outers) * 4 + near % 4

    for k in range(outers):
        arrived(from_near(k))
        sino_copy(from_near(k), mate, f_send.at[outers + k]).start()

    @pl.when(primary)
    def _():
        for k in range(outers):
            for i in range(4):
                spread(lax.rem(outer + k, outers) * 4 + i)

    for k in range(outers):
        arrived(lax.rem(outer + k, outers) * 4 + mate % 4)
        arrived(lax.rem(outer + k, outers) * 4 + 3 - me % 4)
    own.wait()
    filter_rows(all_sino, ramp, tiles, size, bins // size)

    @pl.when(jnp.logical_not(primary))
    def _():
        for g in range(groups):
            coords_arrived(g)

    scale = jnp.float32(math.pi / (own_angles * groups))
    interpolate(all_coords, tiles, out, scale, own_angles)
    for k in range(1, outers):
        sino_copy(me, mate, s_send.at[k]).wait_send()
    for k in range(outers):
        sino_copy(me, mate, n_send.at[k]).wait_send()
    for k in range(2 * outers):
        sino_copy(me, mate, f_send.at[k]).wait_send()
    for j in range(1, share):
        coord_copy(me, mate, half, c_send.at[j]).wait_send()

    @pl.when(jnp.logical_not(primary))
    def _():
        coord_copy(me, mate, half, c_send.at[0]).wait_send()

    @pl.when(primary)
    def _():
        for i in range(groups * (halves - 1)):
            coord_copy(me, mate, half, x_send.at[i]).wait_send()


def shards(sinogram, detector_coord):
    slices, own_angles, bins = sinogram.shape
    local_rows, width = detector_coord.shape[1:]
    groups, halves = lax.axis_size("ang"), lax.axis_size("sl")
    row_share = local_rows * halves // groups
    share = local_rows // row_share
    sino = sinogram.reshape(slices * own_angles, bins)
    coords = detector_coord.reshape(own_angles, share, row_share, width)
    coords = coords.transpose(1, 0, 2, 3).reshape(share, -1, LANES)
    vmem = pl.BlockSpec(memory_space=pltpu.VMEM)
    size = 256
    return pl.pallas_call(
        functools.partial(kernel, groups, halves, own_angles),
        out_shape=jax.ShapeDtypeStruct((row_share, slices, width), jnp.float32),
        in_specs=[vmem] * 2,
        out_specs=vmem,
        scratch_shapes=[
            pltpu.VMEM((groups,) + sino.shape, sino.dtype),
            pltpu.VMEM((groups,) + coords.shape[1:], coords.dtype),
            pltpu.VMEM((2 * (bins // size) - 1, size, size), jnp.bfloat16),
            pltpu.VMEM((groups * slices * own_angles * bins // LANES, LANES), jnp.float32),
            pltpu.SemaphoreType.DMA((1,)),
            pltpu.SemaphoreType.DMA((groups // 4,)),
            pltpu.SemaphoreType.DMA((groups // 4,)),
            pltpu.SemaphoreType.DMA((groups // 2,)),
            pltpu.SemaphoreType.DMA((groups,)),
            pltpu.SemaphoreType.DMA((share,)),
            pltpu.SemaphoreType.DMA((groups * (halves - 1),)),
            pltpu.SemaphoreType.DMA((groups,)),
        ],
        compiler_params=pltpu.CompilerParams(collective_id=0, has_side_effects=True),
    )(sino, coords)


def solution(mesh):
    in_specs = (P("sl", "ang", None), P("ang", "sl", None))
    out_specs = P("ang", "sl", None)
    return jax.shard_map(shards, mesh=mesh, in_specs=in_specs, out_specs=out_specs, check_vma=False)
```

profile of v0, /device:TPU:10, one launch (start us, length us, event | category | flops | bytes accessed | tf_op | source)
XLA Modules:
  0.0 33.9 jit_solution(4327233350399226329)
XLA Ops:
  0.0 0.9 %reshape.10 = s32[2,8,2,512]{3,2,1,0:T(2,128)S(1)} reshape(s32[2,16,512]{2,1,0:T(8,128)} %param.3) | data formatting | bytes 131072 | tf_op jit(solution)/shard_map/reshape | solution.py:237
  0.9 0.0 copy-start
  0.9 0.7 %reshape.11.coords = s32[8,16,128]{2,1,0:T(8,128)} reshape(s32[8,2,2,512]{3,2,1,0:T(2,128)S(1)} %bitcast.3) | data formatting | bytes 131072 | tf_op jit(solution)/shard_map/reshape | solution.py:238
  1.6 0.1 copy-done
  1.7 0.6 %reshape.9.sino = bf16[16,1024]{1,0:T(8,128)(2,1)} reshape(bf16[8,2,1024]{2,1,0:T(2,128)(2,1)S(1)} %copy-done) | data formatting | bytes 65536 | tf_op jit(solution)/shard_map/reshape | solution.py:236
  2.3 30.3 %shard_map.28 = f32[2,8,512]{2,1,0:T(8,128)} custom-call(bf16[16,1024]{1,0:T(8,128)(2,1)} %reshape.9.sino, s32[8,16,128]{2,1,0:T(8,128)} %reshape.11.coords), custom_call_target="tpu_custom_call" | custom-call | tf_op jit(solution)/shard_map/pallas_call | solution.py:241
  32.6 1.4 %copy.7 = f32[2,8,512]{2,1,0:T(8,128)} copy(f32[2,8,512]{2,1,0:T(8,128)} %shard_map.28) | data formatting | bytes 65536
  (1 shorter events, 0.0 us)
Async XLA Ops:
  0.9 0.8 %copy-start = (bf16[8,2,1024]{2,1,0:T(2,128)(2,1)S(1)}, bf16[8,2,1024]{2,1,0:T(2,128)(2,1)}, u32[]{:S(2)}) copy-start(bf16[8,2,1024]{2,1,0:T(2,128)(2,1)} %param.2) | copy-start | bytes 98308
where the time goes:
time: 34.3 us; the launch traced here: 33.9 us
  Pallas kernels  30.3 us (88%)
  local copies, waits for them, and re-layouts  3.64 us (11%)
    pallas_call x1, Pallas kernels, shards(): pl.pallas_call(functools.partial(kernel, groups, halves, own_angles), out...  30.3 us
    unnamed x3, local copies, waits for them, and re-layouts  1.46 us
    reshape x2, local copies, waits for them, and re-layouts, shards(): coords = detector_coord.reshape(own_angles, share, row_share, width)  0.88 us

commit v1 on v0

v1 whole, which is shorter than its diff:
```python
import functools
import math

import jax
import jax.numpy as jnp
from jax import lax
from jax.experimental import pallas as pl
from jax.experimental.pallas import tpu as pltpu
from jax.sharding import PartitionSpec as P

LANES = 128
SUBLANES = 8
CORES = 2
FRACTION_BITS = 20
MESH = pl.DeviceIdType.MESH
ALONG_LANES = lax.GatherDimensionNumbers(
    offset_dims=(),
    collapsed_slice_dims=(1,),
    start_index_map=(1,),
    operand_batching_dims=(0,),
    start_indices_batching_dims=(0,),
)


def build_strip(strip, bins):
    row = lax.broadcasted_iota(jnp.int32, strip.shape, 0)
    lane = lax.broadcasted_iota(jnp.int32, strip.shape, 1)
    offset = lane - row + (bins - LANES)
    wide = offset.astype(jnp.float32)
    square = jnp.maximum(wide * wide, jnp.float32(1.0))
    odd = jnp.where((offset & 1) != 0, jnp.float32(-1.0 / math.pi**2) / square, jnp.float32(0.0))
    strip[...] = jnp.where(offset == 0, jnp.float32(0.25), odd).astype(jnp.bfloat16)


def filter_rows(sino, strip, rows_f, size):
    slices, angles, bins = sino.shape
    rows, count = slices * angles, bins // size
    blocks = [sino[:, :, i * size : (i + 1) * size].reshape(rows, size) for i in range(count)]
    totals = [None] * count
    for d in range(1 - count, count):
        inner = [i for i in range(count) if 0 <= i + d < count]
        first = bins - LANES - size * d
        right = jnp.concatenate(
            [strip[first - u : first - u + size, :] for u in range(0, size, LANES)], axis=1
        )
        left = jnp.concatenate([blocks[i] for i in inner], axis=0)
        part = jnp.dot(left, right, preferred_element_type=jnp.float32)
        for at, i in enumerate(inner):
            piece = part[at * rows : (at + 1) * rows]
            totals[i + d] = piece if totals[i + d] is None else totals[i + d] + piece
    for j, total in enumerate(totals):
        total = total.astype(jnp.bfloat16).astype(jnp.float32)
        for u in range(0, size, LANES):
            at = (j * size + u) // LANES * rows
            rows_f[at : at + rows, :] = total[:, u : u + LANES]


def build_tables(rows_f, tables_f, slices, angles):
    levels = rows_f.shape[0] // (slices * angles)
    bins = levels * LANES
    for a in range(angles):
        starts = [level * slices * angles + a for level in range(levels)]
        here = jnp.concatenate(
            [rows_f[pl.ds(at, slices, stride=angles), :] for at in starts], axis=1
        )
        following = pltpu.roll(here, bins - 1, 1)
        for v, value in enumerate((here, following)):
            for level in range(levels):
                at = pl.ds(level * angles + a, slices, stride=levels * angles)
                tables_f[v, at, :] = value[:, level * LANES : (level + 1) * LANES]


def pick(table, index):
    return lax.gather(
        table, index[..., None], ALONG_LANES, (1, 1),
        mode=lax.GatherScatterMode.PROMISE_IN_BOUNDS,
    )


def spot_weights(lines, group):
    angles = len(lines)
    row = lax.broadcasted_iota(jnp.int32, (SUBLANES, LANES), 0)
    value = jnp.broadcast_to(lines[0], (SUBLANES, LANES))
    for a in range(1, angles):
        value = jnp.where(row % angles == a, jnp.broadcast_to(lines[a], (SUBLANES, LANES)), value)
    left = value >> FRACTION_BITS
    lane, level = left & (LANES - 1), left >> 7
    right_w = (value & (2**FRACTION_BITS - 1)).astype(jnp.float32) * jnp.float32(2.0**-FRACTION_BITS)
    left_w = 1.0 - right_w
    masks = [level == (row + at) // angles for at in range(0, group, SUBLANES)]

    def stack(parts):
        return jnp.concatenate(parts, axis=0)

    return (
        stack([lane] * len(masks)).astype(jnp.int16),
        stack([jnp.where(m, left_w, 0.0) for m in masks]).astype(jnp.bfloat16),
        stack([jnp.where(m, right_w, 0.0) for m in masks]).astype(jnp.bfloat16),
    )


def fold(value):
    value = value.astype(jnp.float32)
    total = value[:SUBLANES]
    for at in range(SUBLANES, value.shape[0], SUBLANES):
        total = total + value[at : at + SUBLANES]
    return total


def spot_sums(tables, lines, slices, sums):
    group = tables.shape[1] // slices
    index, left_w, right_w = spot_weights(lines, group)
    result = []
    for s in range(slices):
        at = slice(s * group, (s + 1) * group)
        value = fold(left_w * pick(tables[0, at, :], index) + right_w * pick(tables[1, at, :], index))
        result.append(value if sums is None else sums[s] + value)
    return result


def add_rows(sums):
    row = lax.broadcasted_iota(jnp.int32, (SUBLANES, LANES), 0)

    def join(a, b, shift):
        low = (row & shift) == 0
        return jnp.where(low, a + pltpu.roll(a, SUBLANES - shift, 0), b + pltpu.roll(b, shift, 0))

    done = []
    for start in range(0, len(sums), SUBLANES):
        part = sums[start : start + SUBLANES]
        part = part + [jnp.zeros_like(part[0])] * (SUBLANES - len(part))
        for shift in (4, 2, 1):
            part = [join(part[i], part[i + shift], shift) for i in range(shift)]
        done.append(part[0])
    done = done[0] if len(done) == 1 else jnp.concatenate(done, axis=0)
    return done[: len(sums)]


def kernel(
    groups, halves, row_share, sino_hbm, coord_hbm, out, sino, strip, rows_f, tables_f, tables,
    coords, stage, early, send, recv, local_sem, t_send, t_recv, c_send, c_recv, p_send, p_recv,
):
    me, half = lax.axis_index("ang"), lax.axis_index("sl")
    core = lax.rem(me, CORES)
    mate = me + 1 - 2 * core
    slices, angles, bins = sino.shape
    tiles, per_tile, columns = coords.shape[3:]
    share = tiles * per_tile // row_share
    across = columns // LANES

    own_side = coord_hbm.at[:, :, :, pl.ds(pl.multiple_of(core * columns, LANES), columns)]
    mate_side = coord_hbm.at[:, :, :, pl.ds(pl.multiple_of((1 - core) * columns, LANES), columns)]
    get_sino = pltpu.make_async_copy(sino_hbm, sino, local_sem.at[0])
    get_own = pltpu.make_async_copy(own_side, coords.at[half, core], local_sem.at[1])
    get_mate = pltpu.make_async_copy(mate_side, stage, local_sem.at[2])
    get_sino.start()
    get_own.start()
    get_mate.start()

    barrier = pltpu.get_barrier_semaphore()

    def signal(ang, sl):
        pl.semaphore_signal(barrier, inc=1, device_id={"ang": ang, "sl": sl}, device_id_type=MESH)

    for k in range(1, groups):
        signal(lax.rem(me + k, groups), half)
    for t in range(1, halves):
        signal(me, lax.rem(half + t, halves))
        signal(mate, lax.rem(half + t, halves))

    build_strip(strip, bins)
    get_sino.wait()
    filter_rows(sino, strip, rows_f, 2 * LANES)
    build_tables(rows_f, tables_f, slices, angles)
    for v in range(2):
        tables[core, v] = tables_f[v].astype(jnp.bfloat16)
    get_own.wait()
    get_mate.wait()
    pl.semaphore_wait(barrier, groups - 1 + CORES * (halves - 1))

    def remote(source, target, send_sem, recv_sem, ang, sl):
        return pltpu.make_async_remote_copy(
            src_ref=source, dst_ref=target, send_sem=send_sem, recv_sem=recv_sem,
            device_id={"ang": ang, "sl": sl}, device_id_type=MESH,
        )

    inputs = [
        remote(tables.at[core], tables.at[core], t_send, t_recv, mate, half),
        remote(stage, coords.at[half, core], c_send.at[0], c_recv.at[half, core], mate, half),
    ]
    for t in range(1, halves):
        side = lax.rem(half + t, halves)
        inputs.append(remote(
            coords.at[half, core], coords.at[half, core], c_send.at[2 * t - 1],
            c_recv.at[half, core], me, side,
        ))
        inputs.append(remote(
            stage, coords.at[half, core], c_send.at[2 * t], c_recv.at[half, core], mate, side,
        ))
    for copy in inputs:
        copy.start()

    def lines(t, k, tile, r, x):
        return [
            coords[t, k, a, tile, r : r + 1, x * LANES : (x + 1) * LANES] for a in range(angles)
        ]

    spots = [(r, x) for r in range(per_tile) for x in range(across)]

    def own_angles(tile, carry):
        for r, x in spots:
            sums = spot_sums(tables.at[core], lines(half, core, tile, r, x), slices, None)
            for s in range(slices):
                early[tile, r * across + x, s] = sums[s]
        return carry

    lax.fori_loop(0, tiles, own_angles, 0)

    def part_copy(owner):
        return remote(
            send.at[owner], recv.at[me], p_send.at[owner], p_recv.at[me], owner, half
        )

    def deliver(t, tile, done):
        for o in range(per_tile // row_share):
            owner = t * share + tile * (per_tile // row_share) + o
            value = jnp.concatenate(
                [
                    jnp.concatenate([done[o * row_share + i, x] for x in range(across)], axis=1)
                    for i in range(row_share)
                ],
                axis=0,
            ).astype(jnp.bfloat16)

            @pl.when(owner == me)
            def _():
                recv[me] = value

            @pl.when(owner != me)
            def _():
                send[owner] = value
                part_copy(owner).start()

    inputs[0].wait_recv()

    def coords_arrived(t, k):
        pltpu.make_async_copy(stage, coords.at[t, k], c_recv.at[t, k]).wait()

    coords_arrived(half, 1 - core)

    def mate_angles(tile, carry):
        done = {}
        for r, x in spots:
            sums = [early[tile, r * across + x, s] for s in range(slices)]
            done[r, x] = add_rows(spot_sums(
                tables.at[1 - core], lines(half, 1 - core, tile, r, x), slices, sums
            ))
        deliver(half, tile, done)
        return carry

    lax.fori_loop(0, tiles, mate_angles, 0)

    for t in range(1, halves):
        side = lax.rem(half + t, halves)
        for k in range(CORES):
            coords_arrived(side, k)

        def all_angles(tile, carry):
            done = {}
            for r, x in spots:
                sums = None
                for k in range(CORES):
                    sums = spot_sums(tables.at[k], lines(side, k, tile, r, x), slices, sums)
                done[r, x] = add_rows(sums)
            deliver(side, tile, done)
            return carry

        lax.fori_loop(0, tiles, all_angles, 0)

    for k in range(1, groups):
        source = lax.rem(me + k, groups)
        remote(send.at[0], recv.at[source], p_send.at[0], p_recv.at[source], mate, half).wait_recv()
    scale = jnp.float32(math.pi / (angles * groups))
    for c in range(CORES):
        total = None
        for chip in range(groups // CORES):
            value = recv[chip * CORES + c].astype(jnp.float32)
            total = value if total is None else total + value
        total = total * scale
        for i in range(row_share):
            out[i, :, c * columns : (c + 1) * columns] = total[i * slices : (i + 1) * slices]
    for copy in inputs:
        copy.wait_send()
    for k in range(1, groups):
        part_copy(lax.rem(me + k, groups)).wait_send()


def shards(sinogram, detector_coord):
    slices, angles, bins = sinogram.shape
    local_rows, width = detector_coord.shape[1:]
    groups, halves = lax.axis_size("ang"), lax.axis_size("sl")
    row_share = local_rows * halves // groups
    tiles, columns = local_rows // SUBLANES, width // CORES
    group = bins // LANES * angles
    coords = detector_coord.reshape(angles, tiles, SUBLANES, width)
    block = (angles, tiles, SUBLANES, columns)
    message = (groups, row_share * slices, columns)
    spots = SUBLANES * columns // LANES
    dma = pltpu.SemaphoreType.DMA
    return pl.pallas_call(
        functools.partial(kernel, groups, halves, row_share),
        out_shape=pltpu.VMEM((row_share, slices, width), jnp.float32),
        in_specs=[pl.BlockSpec(memory_space=pl.ANY)] * 2,
        out_specs=pl.BlockSpec(memory_space=pltpu.VMEM),
        scratch_shapes=[
            pltpu.VMEM(sinogram.shape, sinogram.dtype),
            pltpu.VMEM((2 * bins - LANES, LANES), jnp.bfloat16),
            pltpu.VMEM((slices * group, LANES), jnp.float32),
            pltpu.VMEM((2, slices * group, LANES), jnp.float32),
            pltpu.VMEM((CORES, 2, slices * group, LANES), jnp.bfloat16),
            pltpu.VMEM((halves, CORES) + block, jnp.int32),
            pltpu.VMEM(block, jnp.int32),
            pltpu.VMEM((tiles, spots, slices, SUBLANES, LANES), jnp.float32),
            pltpu.VMEM(message, jnp.bfloat16),
            pltpu.VMEM(message, jnp.bfloat16),
            dma((3,)),
            dma(()),
            dma(()),
            dma((2 * halves - 1,)),
            dma((halves, CORES)),
            dma((groups,)),
            dma((groups,)),
        ],
        compiler_params=pltpu.CompilerParams(collective_id=0, has_side_effects=True),
    )(sinogram, coords)


def solution(mesh):
    in_specs = (P("sl", "ang", None), P("ang", "sl", None))
    out_specs = P("ang", "sl", None)
    return jax.shard_map(shards, mesh=mesh, in_specs=in_specs, out_specs=out_specs, check_vma=False)
```

time: 34.3 us -> 13.9 us (0.41)
  the two profiles are of different devices: /device:TPU:10 before, /device:TPU:0 now
where the time goes in v1:
time: 13.9 us; the launch traced here: 13.7 us
  Pallas kernels  13.1 us (94%)
  local copies, waits for them, and re-layouts  0.62 us (4%)
    pallas_call x1, Pallas kernels, shards(): pl.pallas_call(functools.partial(kernel, groups, halves, row_share), out_...  13.1 us
    unnamed x1, local copies, waits for them, and re-layouts  0.62 us

profile of v1, /device:TPU:0, one launch (start us, length us, event | category | flops | bytes accessed | tf_op | source)
XLA Modules:
  0.0 13.7 jit_solution(13555506512846516873)
XLA Ops:
  0.0 13.1 %shard_map.28 = f32[2,8,512]{2,1,0:T(8,128)S(1)} custom-call(bf16[8,2,1024]{2,1,0:T(2,128)(2,1)} %sino_hbm.1, s32[2,2,8,512]{3,2,1,0:T(8,128)} %bitcast.1), custom_call_target="tpu_custom_call" | custom-call | tf_op jit(solution)/shard_map/pallas_call | solution.py:310
  13.1 0.6 %copy.4 = f32[2,8,512]{2,1,0:T(8,128)} copy(f32[2,8,512]{2,1,0:T(8,128)S(1)} %shard_map.28) | data formatting | bytes 65536

commit v2 on v1

--- a/solution.py
+++ b/solution.py
@@ -138,35 +138,50 @@
 
 def kernel(
     groups, halves, row_share, sino_hbm, coord_hbm, out, sino, strip, rows_f, tables_f, tables,
-    coords, stage, early, send, recv, local_sem, t_send, t_recv, c_send, c_recv, p_send, p_recv,
+    coords, stage, early, send, recv, local_sem, t_send, t_recv, c_send, c_recv, p_send, p_recv, lower_sem, upper_sem,
 ):
     me, half = lax.axis_index("ang"), lax.axis_index("sl")
     core = lax.rem(me, CORES)
     mate = me + 1 - 2 * core
     slices, angles, bins = sino.shape
-    tiles, per_tile, columns = coords.shape[3:]
+    tiles, _, per_tile, columns = coords.shape[2:]
     share = tiles * per_tile // row_share
     across = columns // LANES
 
-    own_side = coord_hbm.at[:, :, :, pl.ds(pl.multiple_of(core * columns, LANES), columns)]
-    mate_side = coord_hbm.at[:, :, :, pl.ds(pl.multiple_of((1 - core) * columns, LANES), columns)]
+    def local_coords(tile, side, target, sem):
+        at = pl.ds(pl.multiple_of(side * columns, LANES), columns)
+        return pltpu.make_async_copy(coord_hbm.at[:, tile, :, at], target.at[tile], local_sem.at[sem])
+
     get_sino = pltpu.make_async_copy(sino_hbm, sino, local_sem.at[0])
-    get_own = pltpu.make_async_copy(own_side, coords.at[half, core], local_sem.at[1])
-    get_mate = pltpu.make_async_copy(mate_side, stage, local_sem.at[2])
+    get_coords = []
+    for tile in range(tiles):
+        get_coords.append(local_coords(tile, core, coords.at[half, core], 2 * tile + 1))
+        get_coords.append(local_coords(tile, 1 - core, stage, 2 * tile + 2))
     get_sino.start()
-    get_own.start()
-    get_mate.start()
-
+    for copy in get_coords:
+        copy.start()
+
+    quad = 2 * CORES
+    place, places = me // quad, groups // quad
     barrier = pltpu.get_barrier_semaphore()
 
-    def signal(ang, sl):
-        pl.semaphore_signal(barrier, inc=1, device_id={"ang": ang, "sl": sl}, device_id_type=MESH)
-
-    for k in range(1, groups):
-        signal(lax.rem(me + k, groups), half)
+    def signal(sem, ang, sl):
+        pl.semaphore_signal(sem, inc=1, device_id={"ang": ang, "sl": sl}, device_id_type=MESH)
+
     for t in range(1, halves):
-        signal(me, lax.rem(half + t, halves))
-        signal(mate, lax.rem(half + t, halves))
+        signal(barrier, me, lax.rem(half + t, halves))
+        signal(barrier, mate, lax.rem(half + t, halves))
+    for k in range(1, quad):
+        signal(barrier, place * quad + lax.rem(me + k, quad), half)
+    has_lower, has_upper = place > 0, place < places - 1
+
+    @pl.when(has_lower)
+    def _():
+        signal(barrier, me - quad, half)
+
+    @pl.when(has_upper)
+    def _():
+        signal(barrier, me + quad, half)
 
     build_strip(strip, bins)
     get_sino.wait()
@@ -174,9 +189,18 @@
     build_tables(rows_f, tables_f, slices, angles)
     for v in range(2):
         tables[core, v] = tables_f[v].astype(jnp.bfloat16)
-    get_own.wait()
-    get_mate.wait()
-    pl.semaphore_wait(barrier, groups - 1 + CORES * (halves - 1))
+    for copy in get_coords:
+        copy.wait()
+    beside = has_lower.astype(jnp.int32) + has_upper.astype(jnp.int32)
+    pl.semaphore_wait(barrier, quad - 1 + CORES * (halves - 1) + beside)
+
+    @pl.when(jnp.logical_and(place == 0, has_upper))
+    def _():
+        signal(lower_sem, me + quad, half)
+
+    @pl.when(jnp.logical_and(place == places - 1, has_lower))
+    def _():
+        signal(upper_sem, me - quad, half)
 
     def remote(source, target, send_sem, recv_sem, ang, sl):
         return pltpu.make_async_remote_copy(
@@ -184,46 +208,71 @@
             device_id={"ang": ang, "sl": sl}, device_id_type=MESH,
         )
 
-    inputs = [
-        remote(tables.at[core], tables.at[core], t_send, t_recv, mate, half),
-        remote(stage, coords.at[half, core], c_send.at[0], c_recv.at[half, core], mate, half),
-    ]
-    for t in range(1, halves):
-        side = lax.rem(half + t, halves)
-        inputs.append(remote(
-            coords.at[half, core], coords.at[half, core], c_send.at[2 * t - 1],
-            c_recv.at[half, core], me, side,
-        ))
-        inputs.append(remote(
-            stage, coords.at[half, core], c_send.at[2 * t], c_recv.at[half, core], mate, side,
-        ))
-    for copy in inputs:
+    def coord_copy(tile, source, ang, t, which):
+        return remote(
+            source.at[tile], coords.at[half, core, tile], c_send.at[tile, t, which],
+            c_recv.at[half, core, tile], ang, lax.rem(half + t, halves),
+        )
+
+    def to_side(tile, t):
+        return [
+            coord_copy(tile, coords.at[half, core], me, t, 0),
+            coord_copy(tile, stage, mate, t, 1),
+        ]
+
+    def start_sides(tiles_now):
+        for tile in tiles_now:
+            for t in range(1, halves):
+                for copy in to_side(tile, t):
+                    copy.start()
+
+    start_sides(range(1))
+    mate_coords = [coord_copy(tile, stage, mate, 0, 1) for tile in range(tiles)]
+    for copy in mate_coords:
         copy.start()
+    mate_tables = remote(tables.at[core], tables.at[core], t_send, t_recv, mate, half)
+    mate_tables.start()
 
     def lines(t, k, tile, r, x):
         return [
-            coords[t, k, a, tile, r : r + 1, x * LANES : (x + 1) * LANES] for a in range(angles)
+            coords[t, k, tile, a, r : r + 1, x * LANES : (x + 1) * LANES] for a in range(angles)
         ]
 
     spots = [(r, x) for r in range(per_tile) for x in range(across)]
+
+    middle = jnp.logical_and(has_lower, has_upper)
 
     def own_angles(tile, carry):
         for r, x in spots:
             sums = spot_sums(tables.at[core], lines(half, core, tile, r, x), slices, None)
             for s in range(slices):
                 early[tile, r * across + x, s] = sums[s]
+
+        @pl.when(jnp.logical_and(tile == jnp.clip(place - 1, 0, tiles - 1), middle))
+        def _():
+            pl.semaphore_wait(lower_sem, 1)
+            signal(lower_sem, me + quad, half)
+
         return carry
 
     lax.fori_loop(0, tiles, own_angles, 0)
+    start_sides(range(1, tiles))
 
     def part_copy(owner):
-        return remote(
-            send.at[owner], recv.at[me], p_send.at[owner], p_recv.at[me], owner, half
-        )
-
-    def deliver(t, tile, done):
-        for o in range(per_tile // row_share):
-            owner = t * share + tile * (per_tile // row_share) + o
+        return remote(send.at[owner], recv.at[me], p_send.at[owner], p_recv.at[me], owner, half)
+
+    per_step = per_tile // row_share
+    steps = halves * tiles
+    beyond = places - 1 - place
+    flush = jnp.where(beyond < 3, jnp.minimum(beyond, tiles) - 1, steps - 1)
+
+    def step_owner(step, o):
+        t, tile = step // tiles, lax.rem(step, tiles)
+        return lax.rem(half + t, halves) * share + tile * per_step + o
+
+    def keep(step, done):
+        for o in range(per_step):
+            owner = step_owner(step, o)
             value = jnp.concatenate(
                 [
                     jnp.concatenate([done[o * row_share + i, x] for x in range(across)], axis=1)
@@ -231,55 +280,86 @@
                 ],
                 axis=0,
             ).astype(jnp.bfloat16)
-
-            @pl.when(owner == me)
+            send[owner] = value
+
+    def deliver(step, upper):
+        for o in range(per_step):
+            owner = step_owner(step, o)
+
+            @pl.when(jnp.logical_and(owner != me, (owner // quad > place) == upper))
             def _():
-                recv[me] = value
-
-            @pl.when(owner != me)
+                part_copy(owner).start()
+
+    def hear(step):
+        @pl.when(jnp.logical_and(flush == step, has_upper))
+        def _():
+            pl.semaphore_wait(upper_sem, 1)
+
+            @pl.when(has_lower)
             def _():
-                send[owner] = value
-                part_copy(owner).start()
-
-    inputs[0].wait_recv()
-
-    def coords_arrived(t, k):
-        pltpu.make_async_copy(stage, coords.at[t, k], c_recv.at[t, k]).wait()
-
-    coords_arrived(half, 1 - core)
+                signal(upper_sem, me - quad, half)
+
+        def late(earlier, carry):
+            deliver(earlier, True)
+            return carry
+
+        lax.fori_loop(jnp.where(flush == step, 0, step), step, late, 0)
+
+    def after(step):
+        deliver(step, False)
+        hear(step)
+
+        @pl.when(flush <= step)
+        def _():
+            deliver(step, True)
+
+    hear(-1)
+    mate_tables.wait_recv()
+
+    def coords_arrived(t, k, tile):
+        pltpu.make_async_copy(stage.at[tile], coords.at[t, k, tile], c_recv.at[t, k, tile]).wait()
 
     def mate_angles(tile, carry):
+        coords_arrived(half, 1 - core, tile)
         done = {}
         for r, x in spots:
             sums = [early[tile, r * across + x, s] for s in range(slices)]
             done[r, x] = add_rows(spot_sums(
                 tables.at[1 - core], lines(half, 1 - core, tile, r, x), slices, sums
             ))
-        deliver(half, tile, done)
+        keep(tile, done)
+
+        @pl.when(tile == 0)
+        def _():
+            @pl.when(jnp.logical_and(has_lower, jnp.logical_not(has_upper)))
+            def _():
+                pl.semaphore_wait(lower_sem, 1)
+
+        after(tile)
         return carry
 
     lax.fori_loop(0, tiles, mate_angles, 0)
 
-    for t in range(1, halves):
-        side = lax.rem(half + t, halves)
+    def all_angles(step, carry):
+        side, tile = lax.rem(half + step // tiles, halves), lax.rem(step, tiles)
         for k in range(CORES):
-            coords_arrived(side, k)
-
-        def all_angles(tile, carry):
-            done = {}
-            for r, x in spots:
-                sums = None
-                for k in range(CORES):
-                    sums = spot_sums(tables.at[k], lines(side, k, tile, r, x), slices, sums)
-                done[r, x] = add_rows(sums)
-            deliver(side, tile, done)
-            return carry
-
-        lax.fori_loop(0, tiles, all_angles, 0)
+            coords_arrived(side, k, tile)
+        done = {}
+        for r, x in spots:
+            sums = None
+            for k in range(CORES):
+                sums = spot_sums(tables.at[k], lines(side, k, tile, r, x), slices, sums)
+            done[r, x] = add_rows(sums)
+        keep(step, done)
+        after(step)
+        return carry
+
+    lax.fori_loop(tiles, steps, all_angles, 0)
 
     for k in range(1, groups):
         source = lax.rem(me + k, groups)
         remote(send.at[0], recv.at[source], p_send.at[0], p_recv.at[source], mate, half).wait_recv()
+    recv[me] = send[me]
     scale = jnp.float32(math.pi / (angles * groups))
     for c in range(CORES):
         total = None
@@ -289,8 +369,13 @@
         total = total * scale
         for i in range(row_share):
             out[i, :, c * columns : (c + 1) * columns] = total[i * slices : (i + 1) * slices]
-    for copy in inputs:
+    mate_tables.wait_send()
+    for copy in mate_coords:
         copy.wait_send()
+    for tile in range(tiles):
+        for t in range(1, halves):
+            for copy in to_side(tile, t):
+                copy.wait_send()
     for k in range(1, groups):
         part_copy(lax.rem(me + k, groups)).wait_send()
 
@@ -303,7 +388,7 @@
     tiles, columns = local_rows // SUBLANES, width // CORES
     group = bins // LANES * angles
     coords = detector_coord.reshape(angles, tiles, SUBLANES, width)
-    block = (angles, tiles, SUBLANES, columns)
+    block = (tiles, angles, SUBLANES, columns)
     message = (groups, row_share * slices, columns)
     spots = SUBLANES * columns // LANES
     dma = pltpu.SemaphoreType.DMA
@@ -323,13 +408,15 @@
             pltpu.VMEM((tiles, spots, slices, SUBLANES, LANES), jnp.float32),
             pltpu.VMEM(message, jnp.bfloat16),
             pltpu.VMEM(message, jnp.bfloat16),
-            dma((3,)),
+            dma((2 * tiles + 1,)),
             dma(()),
             dma(()),
-            dma((2 * halves - 1,)),
-            dma((halves, CORES)),
+            dma((tiles, halves, 2)),
+            dma((halves, CORES, tiles)),
             dma((groups,)),
             dma((groups,)),
+            pltpu.SemaphoreType.REGULAR,
+            pltpu.SemaphoreType.REGULAR,
         ],
         compiler_params=pltpu.CompilerParams(collective_id=0, has_side_effects=True),
     )(sinogram, coords)

time: 13.9 us -> 12.5 us (0.90)
  the two profiles are of different devices: /device:TPU:0 before, /device:TPU:11 now
where the time goes in v2:
time: 12.5 us; the launch traced here: 12.3 us
  Pallas kernels  11.7 us (94%)
  local copies, waits for them, and re-layouts  0.62 us (5%)
    pallas_call x1, Pallas kernels, shards(): pl.pallas_call(functools.partial(kernel, groups, halves, row_share), out_...  11.7 us
    unnamed x1, local copies, waits for them, and re-layouts  0.62 us

profile of v2, /device:TPU:11, one launch (start us, length us, event | category | flops | bytes accessed | tf_op | source)
XLA Modules:
  0.0 12.3 jit_solution(6002494046641028897)
XLA Ops:
  0.0 11.7 %shard_map.28 = f32[2,8,512]{2,1,0:T(8,128)S(1)} custom-call(bf16[8,2,1024]{2,1,0:T(2,128)(2,1)} %sino_hbm.1, s32[2,2,8,512]{3,2,1,0:T(8,128)} %bitcast.1), custom_call_target="tpu_custom_call" | custom-call | tf_op jit(solution)/shard_map/pallas_call | solution.py:395
  11.7 0.6 %copy.4 = f32[2,8,512]{2,1,0:T(8,128)} copy(f32[2,8,512]{2,1,0:T(8,128)S(1)} %shard_map.28) | data formatting | bytes 65536

commit v3 on v2

--- a/solution.py
+++ b/solution.py
@@ -11,6 +11,7 @@
 LANES = 128
 SUBLANES = 8
 CORES = 2
+PARTS = 2
 FRACTION_BITS = 20
 MESH = pl.DeviceIdType.MESH
 ALONG_LANES = lax.GatherDimensionNumbers(
@@ -144,19 +145,22 @@
     core = lax.rem(me, CORES)
     mate = me + 1 - 2 * core
     slices, angles, bins = sino.shape
-    tiles, _, per_tile, columns = coords.shape[2:]
+    tiles, _, per_tile, columns = stage.shape
     share = tiles * per_tile // row_share
     across = columns // LANES
 
-    def local_coords(tile, side, target, sem):
+    def block(t, tile, k):
+        return coords.at[(t * tiles + tile) * CORES + k]
+
+    def local_coords(tile, side, target):
         at = pl.ds(pl.multiple_of(side * columns, LANES), columns)
-        return pltpu.make_async_copy(coord_hbm.at[:, tile, :, at], target.at[tile], local_sem.at[sem])
+        return pltpu.make_async_copy(coord_hbm.at[:, tile, :, at], target, local_sem.at[1])
 
     get_sino = pltpu.make_async_copy(sino_hbm, sino, local_sem.at[0])
     get_coords = []
     for tile in range(tiles):
-        get_coords.append(local_coords(tile, core, coords.at[half, core], 2 * tile + 1))
-        get_coords.append(local_coords(tile, 1 - core, stage, 2 * tile + 2))
+        get_coords.append(local_coords(tile, core, block(half, tile, core)))
+        get_coords.append(local_coords(tile, 1 - core, stage.at[tile]))
     get_sino.start()
     for copy in get_coords:
         copy.start()
@@ -181,7 +185,8 @@
 
     @pl.when(has_upper)
     def _():
-        signal(barrier, me + quad, half)
+        for k in range(quad):
+            signal(barrier, (place + 1) * quad + k, half)
 
     build_strip(strip, bins)
     get_sino.wait()
@@ -189,12 +194,12 @@
     build_tables(rows_f, tables_f, slices, angles)
     for v in range(2):
         tables[core, v] = tables_f[v].astype(jnp.bfloat16)
-    for copy in get_coords:
-        copy.wait()
-    beside = has_lower.astype(jnp.int32) + has_upper.astype(jnp.int32)
+    pair = pl.ds(0, CORES * tiles)
+    pltpu.make_async_copy(coords.at[pair], coords.at[pair], local_sem.at[1]).wait()
+    beside = quad * has_lower.astype(jnp.int32) + has_upper.astype(jnp.int32)
     pl.semaphore_wait(barrier, quad - 1 + CORES * (halves - 1) + beside)
 
-    @pl.when(jnp.logical_and(place == 0, has_upper))
+    @pl.when(jnp.logical_and(place == 1, has_upper))
     def _():
         signal(lower_sem, me + quad, half)
 
@@ -208,16 +213,16 @@
             device_id={"ang": ang, "sl": sl}, device_id_type=MESH,
         )
 
-    def coord_copy(tile, source, ang, t, which):
+    def coord_copy(tile, source, ang, t):
         return remote(
-            source.at[tile], coords.at[half, core, tile], c_send.at[tile, t, which],
-            c_recv.at[half, core, tile], ang, lax.rem(half + t, halves),
+            source, block(half, tile, core), c_send, c_recv.at[half, tile], ang,
+            lax.rem(half + t, halves),
         )
 
     def to_side(tile, t):
         return [
-            coord_copy(tile, coords.at[half, core], me, t, 0),
-            coord_copy(tile, stage, mate, t, 1),
+            coord_copy(tile, block(half, tile, core), me, t),
+            coord_copy(tile, stage.at[tile], mate, t),
         ]
 
     def start_sides(tiles_now):
@@ -227,7 +232,7 @@
                     copy.start()
 
     start_sides(range(1))
-    mate_coords = [coord_copy(tile, stage, mate, 0, 1) for tile in range(tiles)]
+    mate_coords = [coord_copy(tile, stage.at[tile], mate, 0) for tile in range(tiles)]
     for copy in mate_coords:
         copy.start()
     mate_tables = remote(tables.at[core], tables.at[core], t_send, t_recv, mate, half)
@@ -235,12 +240,13 @@
 
     def lines(t, k, tile, r, x):
         return [
-            coords[t, k, tile, a, r : r + 1, x * LANES : (x + 1) * LANES] for a in range(angles)
+            coords[
+                (t * tiles + tile) * CORES + k, a, r : r + 1, x * LANES : (x + 1) * LANES
+            ]
+            for a in range(angles)
         ]
 
     spots = [(r, x) for r in range(per_tile) for x in range(across)]
-
-    middle = jnp.logical_and(has_lower, has_upper)
 
     def own_angles(tile, carry):
         for r, x in spots:
@@ -248,7 +254,7 @@
             for s in range(slices):
                 early[tile, r * across + x, s] = sums[s]
 
-        @pl.when(jnp.logical_and(tile == jnp.clip(place - 1, 0, tiles - 1), middle))
+        @pl.when(jnp.logical_and(tile == 0, jnp.logical_and(place > 1, has_upper)))
         def _():
             pl.semaphore_wait(lower_sem, 1)
             signal(lower_sem, me + quad, half)
@@ -259,7 +265,7 @@
     start_sides(range(1, tiles))
 
     def part_copy(owner):
-        return remote(send.at[owner], recv.at[me], p_send.at[owner], p_recv.at[me], owner, half)
+        return remote(send.at[owner], recv.at[me], p_send, p_recv, owner, half)
 
     per_step = per_tile // row_share
     steps = halves * tiles
@@ -270,23 +276,25 @@
         t, tile = step // tiles, lax.rem(step, tiles)
         return lax.rem(half + t, halves) * share + tile * per_step + o
 
-    def keep(step, done):
-        for o in range(per_step):
-            owner = step_owner(step, o)
+    per_part = max(per_step // PARTS, 1)
+    parts = [range(o, o + per_part) for o in range(0, per_step, per_part)]
+
+    def keep(step, owners, done):
+        for o in owners:
             value = jnp.concatenate(
                 [
                     jnp.concatenate([done[o * row_share + i, x] for x in range(across)], axis=1)
                     for i in range(row_share)
                 ],
                 axis=0,
-            ).astype(jnp.bfloat16)
-            send[owner] = value
-
-    def deliver(step, upper):
-        for o in range(per_step):
+            )
+            send[step_owner(step, o)] = value.astype(jnp.bfloat16)
+
+    def deliver(step, owners, wanted):
+        for o in owners:
             owner = step_owner(step, o)
 
-            @pl.when(jnp.logical_and(owner != me, (owner // quad > place) == upper))
+            @pl.when(jnp.logical_and(owner != me, wanted(owner // quad)))
             def _():
                 part_copy(owner).start()
 
@@ -300,84 +308,85 @@
                 signal(upper_sem, me - quad, half)
 
         def late(earlier, carry):
-            deliver(earlier, True)
+            deliver(earlier, range(per_step), lambda to: to > place)
             return carry
 
-        lax.fori_loop(jnp.where(flush == step, 0, step), step, late, 0)
-
-    def after(step):
-        deliver(step, False)
-        hear(step)
-
-        @pl.when(flush <= step)
+        lax.fori_loop(0, jnp.where(flush == step, step + 1, 0), late, 0)
+
+    def hear_lower(step):
+        @pl.when(jnp.logical_and(step == 0, jnp.logical_and(place > 1, jnp.logical_not(has_upper))))
         def _():
-            deliver(step, True)
+            pl.semaphore_wait(lower_sem, 1)
+
+    def run_step(step, sums_of, first):
+        for owners in parts:
+            done = {}
+            for o in owners:
+                for i in range(row_share):
+                    for x in range(across):
+                        r = o * row_share + i
+                        done[r, x] = add_rows(sums_of(r, x))
+            keep(step, owners, done)
+            if first and owners is parts[0]:
+                hear_lower(step)
+            deliver(step, owners, lambda to: jnp.logical_or(to <= place, flush < step))
 
     hear(-1)
     mate_tables.wait_recv()
 
-    def coords_arrived(t, k, tile):
-        pltpu.make_async_copy(stage.at[tile], coords.at[t, k, tile], c_recv.at[t, k, tile]).wait()
+    def coords_arrived(t, tile, count):
+        at = pl.ds((t * tiles + tile) * CORES, count)
+        pltpu.make_async_copy(coords.at[at], coords.at[at], c_recv.at[t, tile]).wait()
 
     def mate_angles(tile, carry):
-        coords_arrived(half, 1 - core, tile)
-        done = {}
-        for r, x in spots:
+        coords_arrived(half, tile, 1)
+
+        def sums_of(r, x):
             sums = [early[tile, r * across + x, s] for s in range(slices)]
-            done[r, x] = add_rows(spot_sums(
+            return spot_sums(
                 tables.at[1 - core], lines(half, 1 - core, tile, r, x), slices, sums
-            ))
-        keep(tile, done)
-
-        @pl.when(tile == 0)
-        def _():
-            @pl.when(jnp.logical_and(has_lower, jnp.logical_not(has_upper)))
-            def _():
-                pl.semaphore_wait(lower_sem, 1)
-
-        after(tile)
+            )
+
+        run_step(tile, sums_of, True)
+        hear(tile)
         return carry
 
     lax.fori_loop(0, tiles, mate_angles, 0)
 
     def all_angles(step, carry):
         side, tile = lax.rem(half + step // tiles, halves), lax.rem(step, tiles)
-        for k in range(CORES):
-            coords_arrived(side, k, tile)
-        done = {}
-        for r, x in spots:
+        coords_arrived(side, tile, CORES)
+
+        def sums_of(r, x):
             sums = None
             for k in range(CORES):
                 sums = spot_sums(tables.at[k], lines(side, k, tile, r, x), slices, sums)
-            done[r, x] = add_rows(sums)
-        keep(step, done)
-        after(step)
+            return sums
+
+        run_step(step, sums_of, False)
+        hear(step)
         return carry
 
     lax.fori_loop(tiles, steps, all_angles, 0)
 
-    for k in range(1, groups):
-        source = lax.rem(me + k, groups)
-        remote(send.at[0], recv.at[source], p_send.at[0], p_recv.at[source], mate, half).wait_recv()
+    others = pl.ds(0, groups - 1)
+    everyone = remote(send.at[others], recv.at[others], p_send, p_recv, mate, half)
+    everyone.wait_recv()
     recv[me] = send[me]
+    totals = [None] * CORES
+    for source in range(groups):
+        value = recv[source].astype(jnp.float32)
+        c = source % CORES
+        totals[c] = value if totals[c] is None else totals[c] + value
     scale = jnp.float32(math.pi / (angles * groups))
     for c in range(CORES):
-        total = None
-        for chip in range(groups // CORES):
-            value = recv[chip * CORES + c].astype(jnp.float32)
-            total = value if total is None else total + value
-        total = total * scale
+        total = totals[c] * scale
         for i in range(row_share):
             out[i, :, c * columns : (c + 1) * columns] = total[i * slices : (i + 1) * slices]
     mate_tables.wait_send()
-    for copy in mate_coords:
-        copy.wait_send()
-    for tile in range(tiles):
-        for t in range(1, halves):
-            for copy in to_side(tile, t):
-                copy.wait_send()
-    for k in range(1, groups):
-        part_copy(lax.rem(me + k, groups)).wait_send()
+    given = coords.at[pl.ds(0, tiles * (1 + CORES * (halves - 1)))]
+    remote(given, given, c_send, c_recv.at[0, 0], mate, half).wait_send()
+    everyone.wait_send()
 
 
 def shards(sinogram, detector_coord):
@@ -388,7 +397,7 @@
     tiles, columns = local_rows // SUBLANES, width // CORES
     group = bins // LANES * angles
     coords = detector_coord.reshape(angles, tiles, SUBLANES, width)
-    block = (tiles, angles, SUBLANES, columns)
+    block = (angles, SUBLANES, columns)
     message = (groups, row_share * slices, columns)
     spots = SUBLANES * columns // LANES
     dma = pltpu.SemaphoreType.DMA
@@ -403,18 +412,18 @@
             pltpu.VMEM((slices * group, LANES), jnp.float32),
             pltpu.VMEM((2, slices * group, LANES), jnp.float32),
             pltpu.VMEM((CORES, 2, slices * group, LANES), jnp.bfloat16),
-            pltpu.VMEM((halves, CORES) + block, jnp.int32),
-            pltpu.VMEM(block, jnp.int32),
+            pltpu.VMEM((halves * tiles * CORES,) + block, jnp.int32),
+            pltpu.VMEM((tiles,) + block, jnp.int32),
             pltpu.VMEM((tiles, spots, slices, SUBLANES, LANES), jnp.float32),
             pltpu.VMEM(message, jnp.bfloat16),
             pltpu.VMEM(message, jnp.bfloat16),
-            dma((2 * tiles + 1,)),
+            dma((2,)),
             dma(()),
             dma(()),
-            dma((tiles, halves, 2)),
-            dma((halves, CORES, tiles)),
-            dma((groups,)),
-            dma((groups,)),
+            dma(()),
+            dma((halves, tiles)),
+            dma(()),
+            dma(()),
             pltpu.SemaphoreType.REGULAR,
             pltpu.SemaphoreType.REGULAR,
         ],

time: 12.5 us -> 11.9 us (0.952)
  the two profiles are of different devices: /device:TPU:11 before, /device:TPU:0 now
where the time goes in v3:
time: 11.9 us; the launch traced here: 11.7 us
  Pallas kernels  11.1 us (93%)
  local copies, waits for them, and re-layouts  0.62 us (5%)
    pallas_call x1, Pallas kernels, shards(): pl.pallas_call(functools.partial(kernel, groups, halves, row_share), out_...  11.1 us
    unnamed x1, local copies, waits for them, and re-layouts  0.62 us

profile of v3, /device:TPU:0, one launch (start us, length us, event | category | flops | bytes accessed | tf_op | source)
XLA Modules:
  0.0 11.7 jit_solution(13020533069224116411)
XLA Ops:
  0.0 11.1 %shard_map.28 = f32[2,8,512]{2,1,0:T(8,128)S(1)} custom-call(bf16[8,2,1024]{2,1,0:T(2,128)(2,1)} %sino_hbm.1, s32[2,2,8,512]{3,2,1,0:T(8,128)} %bitcast.1), custom_call_target="tpu_custom_call" | custom-call | tf_op jit(solution)/shard_map/pallas_call | solution.py:404
  11.1 0.6 %copy.4 = f32[2,8,512]{2,1,0:T(8,128)} copy(f32[2,8,512]{2,1,0:T(8,128)S(1)} %shard_map.28) | data formatting | bytes 65536

commit v4 on v3

--- a/solution.py
+++ b/solution.py
@@ -139,31 +139,26 @@
 
 def kernel(
     groups, halves, row_share, sino_hbm, coord_hbm, out, sino, strip, rows_f, tables_f, tables,
-    coords, stage, early, send, recv, local_sem, t_send, t_recv, c_send, c_recv, p_send, p_recv, lower_sem, upper_sem,
+    raw, coords, stage, early, send, recv, local_sem, t_send, t_recv, c_send, c_recv, p_send, p_recv, lower_sem, next_sem, upper_sem,
 ):
     me, half = lax.axis_index("ang"), lax.axis_index("sl")
     core = lax.rem(me, CORES)
     mate = me + 1 - 2 * core
     slices, angles, bins = sino.shape
-    tiles, _, per_tile, columns = stage.shape
+    tiles, per_tile, width = raw.shape[1:]
+    columns = width // CORES
     share = tiles * per_tile // row_share
     across = columns // LANES
-
-    def block(t, tile, k):
-        return coords.at[(t * tiles + tile) * CORES + k]
-
-    def local_coords(tile, side, target):
-        at = pl.ds(pl.multiple_of(side * columns, LANES), columns)
-        return pltpu.make_async_copy(coord_hbm.at[:, tile, :, at], target, local_sem.at[1])
+    per_step = per_tile // row_share
+    part_rows = per_tile // PARTS
+
+    def block(t, tile, part, k):
+        return ((t * tiles + tile) * PARTS + part) * CORES + k
 
     get_sino = pltpu.make_async_copy(sino_hbm, sino, local_sem.at[0])
-    get_coords = []
-    for tile in range(tiles):
-        get_coords.append(local_coords(tile, core, block(half, tile, core)))
-        get_coords.append(local_coords(tile, 1 - core, stage.at[tile]))
+    get_coords = pltpu.make_async_copy(coord_hbm, raw, local_sem.at[1])
     get_sino.start()
-    for copy in get_coords:
-        copy.start()
+    get_coords.start()
 
     quad = 2 * CORES
     place, places = me // quad, groups // quad
@@ -194,8 +189,19 @@
     build_tables(rows_f, tables_f, slices, angles)
     for v in range(2):
         tables[core, v] = tables_f[v].astype(jnp.bfloat16)
-    pair = pl.ds(0, CORES * tiles)
-    pltpu.make_async_copy(coords.at[pair], coords.at[pair], local_sem.at[1]).wait()
+    get_coords.wait()
+    own_side, mate_side = (
+        pl.ds(pl.multiple_of(c * columns, LANES), columns) for c in (core, 1 - core)
+    )
+    for tile in range(tiles):
+        for part in range(PARTS):
+            at = slice(part * part_rows, (part + 1) * part_rows)
+            coords[block(half, tile, part, core)] = jnp.concatenate(
+                [raw[a, tile, at, own_side] for a in range(angles)], axis=0
+            )
+            stage[tile * PARTS + part] = jnp.concatenate(
+                [raw[a, tile, at, mate_side] for a in range(angles)], axis=0
+            )
     beside = quad * has_lower.astype(jnp.int32) + has_upper.astype(jnp.int32)
     pl.semaphore_wait(barrier, quad - 1 + CORES * (halves - 1) + beside)
 
@@ -203,9 +209,9 @@
     def _():
         signal(lower_sem, me + quad, half)
 
-    @pl.when(jnp.logical_and(place == places - 1, has_lower))
+    @pl.when(has_lower)
     def _():
-        signal(upper_sem, me - quad, half)
+        signal(next_sem, me - quad, half)
 
     def remote(source, target, send_sem, recv_sem, ang, sl):
         return pltpu.make_async_remote_copy(
@@ -213,35 +219,31 @@
             device_id={"ang": ang, "sl": sl}, device_id_type=MESH,
         )
 
-    def coord_copy(tile, source, ang, t):
+    def coord_copy(tile, part, source, ang, t):
         return remote(
-            source, block(half, tile, core), c_send, c_recv.at[half, tile], ang,
-            lax.rem(half + t, halves),
+            source, coords.at[block(half, tile, part, core)], c_send, c_recv.at[half, tile, part],
+            ang, lax.rem(half + t, halves),
         )
 
-    def to_side(tile, t):
-        return [
-            coord_copy(tile, block(half, tile, core), me, t),
-            coord_copy(tile, stage.at[tile], mate, t),
-        ]
-
-    def start_sides(tiles_now):
-        for tile in tiles_now:
-            for t in range(1, halves):
-                for copy in to_side(tile, t):
-                    copy.start()
-
-    start_sides(range(1))
-    mate_coords = [coord_copy(tile, stage.at[tile], mate, 0) for tile in range(tiles)]
-    for copy in mate_coords:
-        copy.start()
+    def start_sides(tile, part):
+        for t in range(1, halves):
+            mine = coords.at[block(half, tile, part, core)]
+            coord_copy(tile, part, mine, me, t).start()
+            coord_copy(tile, part, stage.at[tile * PARTS + part], mate, t).start()
+
+    chunks = [(tile, part) for tile in range(tiles) for part in range(PARTS)]
+    start_sides(*chunks[0])
+    for tile, part in chunks:
+        coord_copy(tile, part, stage.at[tile * PARTS + part], mate, 0).start()
     mate_tables = remote(tables.at[core], tables.at[core], t_send, t_recv, mate, half)
     mate_tables.start()
 
     def lines(t, k, tile, r, x):
+        part, at = r // part_rows, r % part_rows
         return [
             coords[
-                (t * tiles + tile) * CORES + k, a, r : r + 1, x * LANES : (x + 1) * LANES
+                block(t, tile, part, k), a * part_rows + at : a * part_rows + at + 1,
+                x * LANES : (x + 1) * LANES,
             ]
             for a in range(angles)
         ]
@@ -254,6 +256,10 @@
             for s in range(slices):
                 early[tile, r * across + x, s] = sums[s]
 
+        @pl.when(tile == 0)
+        def _():
+            start_sides(*chunks[1])
+
         @pl.when(jnp.logical_and(tile == 0, jnp.logical_and(place > 1, has_upper)))
         def _():
             pl.semaphore_wait(lower_sem, 1)
@@ -262,22 +268,24 @@
         return carry
 
     lax.fori_loop(0, tiles, own_angles, 0)
-    start_sides(range(1, tiles))
+    for chunk in chunks[2:3]:
+        start_sides(*chunk)
 
     def part_copy(owner):
         return remote(send.at[owner], recv.at[me], p_send, p_recv, owner, half)
 
-    per_step = per_tile // row_share
     steps = halves * tiles
     beyond = places - 1 - place
-    flush = jnp.where(beyond < 3, jnp.minimum(beyond, tiles) - 1, steps - 1)
+    near_step = jnp.where(place == 0, tiles - 1, 0)
+    far_step = jnp.where(beyond <= 2, min(tiles, steps - 1), steps - 1)
+    has_far = beyond > 1
 
     def step_owner(step, o):
         t, tile = step // tiles, lax.rem(step, tiles)
         return lax.rem(half + t, halves) * share + tile * per_step + o
 
-    per_part = max(per_step // PARTS, 1)
-    parts = [range(o, o + per_part) for o in range(0, per_step, per_part)]
+    per_part = per_step // PARTS
+    parts = [range(part * per_part, (part + 1) * per_part) for part in range(PARTS)]
 
     def keep(step, owners, done):
         for o in owners:
@@ -298,28 +306,47 @@
             def _():
                 part_copy(owner).start()
 
+    def tell_lower():
+        @pl.when(has_lower)
+        def _():
+            signal(upper_sem, me - quad, half)
+
+    def late(now, step, wanted):
+        def one_step(earlier, carry):
+            deliver(earlier, range(per_step), wanted)
+            return carry
+
+        lax.fori_loop(0, jnp.where(now, step + 1, 0), one_step, 0)
+
     def hear(step):
-        @pl.when(jnp.logical_and(flush == step, has_upper))
+        now = jnp.logical_and(near_step == step, has_upper)
+
+        @pl.when(now)
+        def _():
+            pl.semaphore_wait(next_sem, 1)
+
+            @pl.when(jnp.logical_not(has_far))
+            def _():
+                tell_lower()
+
+        late(now, step, lambda to: to == place + 1)
+        now = jnp.logical_and(far_step == step, has_far)
+
+        @pl.when(now)
         def _():
             pl.semaphore_wait(upper_sem, 1)
-
-            @pl.when(has_lower)
-            def _():
-                signal(upper_sem, me - quad, half)
-
-        def late(earlier, carry):
-            deliver(earlier, range(per_step), lambda to: to > place)
-            return carry
-
-        lax.fori_loop(0, jnp.where(flush == step, step + 1, 0), late, 0)
+            tell_lower()
+
+        late(now, step, lambda to: to > place + 1)
 
     def hear_lower(step):
         @pl.when(jnp.logical_and(step == 0, jnp.logical_and(place > 1, jnp.logical_not(has_upper))))
         def _():
             pl.semaphore_wait(lower_sem, 1)
 
-    def run_step(step, sums_of, first):
-        for owners in parts:
+    def run_step(step, arrived, sums_of, first):
+        for part, owners in enumerate(parts):
+            arrived(part)
             done = {}
             for o in owners:
                 for i in range(row_share):
@@ -327,19 +354,23 @@
                         r = o * row_share + i
                         done[r, x] = add_rows(sums_of(r, x))
             keep(step, owners, done)
-            if first and owners is parts[0]:
+            if first and part == 0:
                 hear_lower(step)
-            deliver(step, owners, lambda to: jnp.logical_or(to <= place, flush < step))
-
-    hear(-1)
+            heard = place + (near_step < step).astype(jnp.int32)
+            heard = jnp.where(far_step < step, places, heard)
+            deliver(step, owners, lambda to: to <= heard)
+
     mate_tables.wait_recv()
-
-    def coords_arrived(t, tile, count):
-        at = pl.ds((t * tiles + tile) * CORES, count)
-        pltpu.make_async_copy(coords.at[at], coords.at[at], c_recv.at[t, tile]).wait()
+    for chunk in chunks[3:]:
+        start_sides(*chunk)
+
+    def coords_arrived(t, tile, part, count):
+        at = pl.ds(block(t, tile, part, 0), count)
+        pltpu.make_async_copy(coords.at[at], coords.at[at], c_recv.at[t, tile, part]).wait()
 
     def mate_angles(tile, carry):
-        coords_arrived(half, tile, 1)
+        def arrived(part):
+            coords_arrived(half, tile, part, 1)
 
         def sums_of(r, x):
             sums = [early[tile, r * across + x, s] for s in range(slices)]
@@ -347,7 +378,7 @@
                 tables.at[1 - core], lines(half, 1 - core, tile, r, x), slices, sums
             )
 
-        run_step(tile, sums_of, True)
+        run_step(tile, arrived, sums_of, True)
         hear(tile)
         return carry
 
@@ -355,7 +386,9 @@
 
     def all_angles(step, carry):
         side, tile = lax.rem(half + step // tiles, halves), lax.rem(step, tiles)
-        coords_arrived(side, tile, CORES)
+
+        def arrived(part):
+            coords_arrived(side, tile, part, CORES)
 
         def sums_of(r, x):
             sums = None
@@ -363,7 +396,7 @@
                 sums = spot_sums(tables.at[k], lines(side, k, tile, r, x), slices, sums)
             return sums
 
-        run_step(step, sums_of, False)
+        run_step(step, arrived, sums_of, False)
         hear(step)
         return carry
 
@@ -384,8 +417,8 @@
         for i in range(row_share):
             out[i, :, c * columns : (c + 1) * columns] = total[i * slices : (i + 1) * slices]
     mate_tables.wait_send()
-    given = coords.at[pl.ds(0, tiles * (1 + CORES * (halves - 1)))]
-    remote(given, given, c_send, c_recv.at[0, 0], mate, half).wait_send()
+    given = coords.at[pl.ds(0, len(chunks) * (1 + CORES * (halves - 1)))]
+    remote(given, given, c_send, c_recv.at[0, 0, 0], mate, half).wait_send()
     everyone.wait_send()
 
 
@@ -397,7 +430,7 @@
     tiles, columns = local_rows // SUBLANES, width // CORES
     group = bins // LANES * angles
     coords = detector_coord.reshape(angles, tiles, SUBLANES, width)
-    block = (angles, SUBLANES, columns)
+    block = (angles * SUBLANES // PARTS, columns)
     message = (groups, row_share * slices, columns)
     spots = SUBLANES * columns // LANES
     dma = pltpu.SemaphoreType.DMA
@@ -412,8 +445,9 @@
             pltpu.VMEM((slices * group, LANES), jnp.float32),
             pltpu.VMEM((2, slices * group, LANES), jnp.float32),
             pltpu.VMEM((CORES, 2, slices * group, LANES), jnp.bfloat16),
-            pltpu.VMEM((halves * tiles * CORES,) + block, jnp.int32),
-            pltpu.VMEM((tiles,) + block, jnp.int32),
+            pltpu.VMEM(coords.shape, jnp.int32),
+            pltpu.VMEM((halves * tiles * PARTS * CORES,) + block, jnp.int32),
+            pltpu.VMEM((tiles * PARTS,) + block, jnp.int32),
             pltpu.VMEM((tiles, spots, slices, SUBLANES, LANES), jnp.float32),
             pltpu.VMEM(message, jnp.bfloat16),
             pltpu.VMEM(message, jnp.bfloat16),
@@ -421,9 +455,10 @@
             dma(()),
             dma(()),
             dma(()),
-            dma((halves, tiles)),
+            dma((halves, tiles, PARTS)),
             dma(()),
             dma(()),
+            pltpu.SemaphoreType.REGULAR,
             pltpu.SemaphoreType.REGULAR,
             pltpu.SemaphoreType.REGULAR,
         ],

time: 11.9 us -> 11.6 us (0.975)
  the two profiles are of different devices: /device:TPU:0 before, /device:TPU:11 now
where the time goes in v4:
time: 11.6 us; the launch traced here: 11.5 us
  Pallas kernels  10.8 us (93%)
  local copies, waits for them, and re-layouts  0.62 us (5%)
    pallas_call x1, Pallas kernels, shards(): pl.pallas_call(functools.partial(kernel, groups, halves, row_share), out_...  10.8 us
    unnamed x1, local copies, waits for them, and re-layouts  0.62 us

profile of v4, /device:TPU:11, one launch (start us, length us, event | category | flops | bytes accessed | tf_op | source)
XLA Modules:
  0.0 11.5 jit_solution(16811218919217677490)
XLA Ops:
  0.0 10.8 %shard_map.28 = f32[2,8,512]{2,1,0:T(8,128)S(1)} custom-call(bf16[8,2,1024]{2,1,0:T(2,128)(2,1)} %sino_hbm.1, s32[2,2,8,512]{3,2,1,0:T(8,128)} %bitcast.1), custom_call_target="tpu_custom_call" | custom-call | tf_op jit(solution)/shard_map/pallas_call | solution.py:437
  10.8 0.6 %copy.4 = f32[2,8,512]{2,1,0:T(8,128)} copy(f32[2,8,512]{2,1,0:T(8,128)S(1)} %shard_map.28) | data formatting | bytes 65536

commit v5 on v4

--- a/solution.py
+++ b/solution.py
@@ -313,7 +313,7 @@
 
     def late(now, step, wanted):
         def one_step(earlier, carry):
-            deliver(earlier, range(per_step), wanted)
+            deliver(step - earlier, range(per_step), wanted)
             return carry
 
         lax.fori_loop(0, jnp.where(now, step + 1, 0), one_step, 0)

time: 11.6 us -> 11.6 us (level)
  the two profiles are of different devices: /device:TPU:11 before, /device:TPU:17 now
where the time goes in v5:
time: 11.6 us; the launch traced here: 11.5 us
  Pallas kernels  10.8 us (93%)
  local copies, waits for them, and re-layouts  0.62 us (5%)
    pallas_call x1, Pallas kernels, shards(): pl.pallas_call(functools.partial(kernel, groups, halves, row_share), out_...  10.8 us
    unnamed x1, local copies, waits for them, and re-layouts  0.62 us

profile of v5, /device:TPU:17, one launch (start us, length us, event | category | flops | bytes accessed | tf_op | source)
XLA Modules:
  0.0 11.5 jit_solution(14354215285814264135)
XLA Ops:
  0.0 10.8 %shard_map.28 = f32[2,8,512]{2,1,0:T(8,128)S(1)} custom-call(bf16[8,2,1024]{2,1,0:T(2,128)(2,1)} %sino_hbm.1, s32[2,2,8,512]{3,2,1,0:T(8,128)} %bitcast.1), custom_call_target="tpu_custom_call" | custom-call | tf_op jit(solution)/shard_map/pallas_call | solution.py:437
  10.8 0.6 %copy.4 = f32[2,8,512]{2,1,0:T(8,128)} copy(f32[2,8,512]{2,1,0:T(8,128)S(1)} %shard_map.28) | data formatting | bytes 65536

commit v6 on v5

--- a/solution.py
+++ b/solution.py
@@ -299,7 +299,7 @@
             send[step_owner(step, o)] = value.astype(jnp.bfloat16)
 
     def deliver(step, owners, wanted):
-        for o in owners:
+        for o in sorted(owners, key=lambda o: o ^ 1):
             owner = step_owner(step, o)
 
             @pl.when(jnp.logical_and(owner != me, wanted(owner // quad)))

time: 11.6 us -> 11.6 us (level)
  the two profiles are of different devices: /device:TPU:17 before, /device:TPU:0 now
where the time goes in v6:
time: 11.6 us; the launch traced here: 11.4 us
  Pallas kernels  10.8 us (93%)
  local copies, waits for them, and re-layouts  0.62 us (5%)
    pallas_call x1, Pallas kernels, shards(): pl.pallas_call(functools.partial(kernel, groups, halves, row_share), out_...  10.8 us
    unnamed x1, local copies, waits for them, and re-layouts  0.62 us

profile of v6, /device:TPU:0, one launch (start us, length us, event | category | flops | bytes accessed | tf_op | source)
XLA Modules:
  0.0 11.4 jit_solution(15252737256448147505)
XLA Ops:
  0.0 10.8 %shard_map.28 = f32[2,8,512]{2,1,0:T(8,128)S(1)} custom-call(bf16[8,2,1024]{2,1,0:T(2,128)(2,1)} %sino_hbm.1, s32[2,2,8,512]{3,2,1,0:T(8,128)} %bitcast.1), custom_call_target="tpu_custom_call" | custom-call | tf_op jit(solution)/shard_map/pallas_call | solution.py:437
  10.8 0.6 %copy.4 = f32[2,8,512]{2,1,0:T(8,128)} copy(f32[2,8,512]{2,1,0:T(8,128)S(1)} %shard_map.28) | data formatting | bytes 65536

commit v7 on v6

--- a/solution.py
+++ b/solution.py
@@ -404,8 +404,8 @@
 
     others = pl.ds(0, groups - 1)
     everyone = remote(send.at[others], recv.at[others], p_send, p_recv, mate, half)
+    recv[me] = send[me]
     everyone.wait_recv()
-    recv[me] = send[me]
     totals = [None] * CORES
     for source in range(groups):
         value = recv[source].astype(jnp.float32)

time: 11.6 us -> 11.6 us (level)
  no operation moved by 1% of the time
where the time goes in v7:
time: 11.6 us; the launch traced here: 11.4 us
  Pallas kernels  10.8 us (93%)
  local copies, waits for them, and re-layouts  0.62 us (5%)
    pallas_call x1, Pallas kernels, shards(): pl.pallas_call(functools.partial(kernel, groups, halves, row_share), out_...  10.8 us
    unnamed x1, local copies, waits for them, and re-layouts  0.62 us

profile of v7, /device:TPU:0, one launch (start us, length us, event | category | flops | bytes accessed | tf_op | source)
XLA Modules:
  0.0 11.4 jit_solution(14042011369542760083)
XLA Ops:
  0.0 10.8 %shard_map.28 = f32[2,8,512]{2,1,0:T(8,128)S(1)} custom-call(bf16[8,2,1024]{2,1,0:T(2,128)(2,1)} %sino_hbm.1, s32[2,2,8,512]{3,2,1,0:T(8,128)} %bitcast.1), custom_call_target="tpu_custom_call" | custom-call | tf_op jit(solution)/shard_map/pallas_call | solution.py:437
  10.8 0.6 %copy.4 = f32[2,8,512]{2,1,0:T(8,128)} copy(f32[2,8,512]{2,1,0:T(8,128)S(1)} %shard_map.28) | data formatting | bytes 65536
